TPU v7x, 128 devices: a whole 4x4x4 slice. The times are simulated.
128 devices in a mesh: slab: 2 (over y_hi), pencil: 64 (over x, y_lo, z, core).
Axes of the slice: x: 4, y: 4 (y_hi: 2, y_lo: 2; y = y_hi * 2 + y_lo), z: 4, core: 2. Of those that a mesh axis runs over, the one named last changes fastest.
Arguments:
- concentration: float32 [512, 512, 256], P('slab', 'pencil'), may hold values from -2 to 2.8
Outputs:
- updated: float32 [512, 512, 256], P('slab', 'pencil')
- mass: float32 [], replicated
All inputs are finite; a program needn't handle non-finite values.
Results may differ from a plain program's by a relative error of at most 0.0002.
Values sent between devices are 32-bit elements; how exact they have to be, the bound alone decides.
A program may use at most 128 MiB of HBM per device.

v0:
```python
import functools
import math

import jax
import jax.numpy as jnp
from jax import lax
from jax.sharding import Mesh
from jax.sharding import PartitionSpec as P

NX = 512
NY = 512
NZ = 256
PENCIL = ("pencil_0", "pencil_1", "pencil_2", "pencil_3")
SLAB_PENCIL = ("slab", "pencil_0", "pencil_1", "pencil_2", "pencil_3")


time_step = 1.0
stiffness = 1.0


def by_axis(x, axes):
    return functools.reduce(lax.psum, axes, x)


def twiddle_tables(length):
    index = jnp.arange(length, dtype=jnp.int32)
    product = index[:, None] * index[None, :] % length
    angle = 2.0 * math.pi / length * product.astype(jnp.float32)
    return (jnp.cos(angle), jnp.sin(angle))


def wavenumber(index, length):
    signed = jnp.where(index < length // 2, index, index - length)
    return 2.0 * math.pi / length * signed.astype(jnp.float32)


def last_forward(field, cosines, sines):
    length = field.shape[-1]
    flat = field.reshape(-1, length)
    real_part = jnp.dot(flat, cosines, precision=lax.Precision.HIGHEST)
    imag_part = -jnp.dot(flat, sines, precision=lax.Precision.HIGHEST)
    shape = field.shape[:-1] + (cosines.shape[1],)
    return (real_part.reshape(shape), imag_part.reshape(shape))


def last_inverse_real(real_part, imag_part, cosines, sines):
    length = real_part.shape[-1]
    flat_real = real_part.reshape(-1, length)
    flat_imag = imag_part.reshape(-1, length)
    result = jnp.dot(flat_real, cosines, precision=lax.Precision.HIGHEST) - jnp.dot(
        flat_imag, sines, precision=lax.Precision.HIGHEST
    )
    return result.reshape(real_part.shape[:-1] + (cosines.shape[1],))


def transform_axis(real_part, imag_part, cosines, sines, form, inverse):
    cos_real = jnp.einsum(form, cosines, real_part, precision=lax.Precision.HIGHEST)
    cos_imag = jnp.einsum(form, cosines, imag_part, precision=lax.Precision.HIGHEST)
    sin_real = jnp.einsum(form, sines, real_part, precision=lax.Precision.HIGHEST)
    sin_imag = jnp.einsum(form, sines, imag_part, precision=lax.Precision.HIGHEST)
    if inverse:
        return (cos_real - sin_imag, cos_imag + sin_real)
    return (cos_real + sin_imag, cos_imag - sin_real)


def local(concentration):
    cube = concentration * concentration * concentration
    depth_cos, depth_sin = twiddle_tables(NZ)
    column_cos, column_sin = twiddle_tables(NY)
    row_cos, row_sin = twiddle_tables(NX)
    columns_kept = NZ // 2
    forward_cos = depth_cos[:, :columns_kept]
    forward_sin = depth_sin[:, :columns_kept]
    weights = jnp.where(jnp.arange(columns_kept, dtype=jnp.int32) == 0, 1.0, 2.0).astype(
        jnp.float32
    )
    inverse_cos = weights[:, None] * depth_cos[:columns_kept, :]
    inverse_sin = weights[:, None] * depth_sin[:columns_kept, :]
    moved = (
        lax.all_to_all(concentration, PENCIL, split_axis=0, concat_axis=1, tiled=True),
        lax.all_to_all(cube, PENCIL, split_axis=0, concat_axis=1, tiled=True),
    )
    conc_real, conc_imag = last_forward(moved[0], forward_cos, forward_sin)
    cube_real, cube_imag = last_forward(moved[1], forward_cos, forward_sin)
    parts = (conc_real, conc_imag, cube_real, cube_imag)
    fields = transform_axis(
        parts[0], parts[1], column_cos, column_sin, "ky,ayz->akz", False
    ) + transform_axis(parts[2], parts[3], column_cos, column_sin, "ky,ayz->akz", False)
    parts = (
        lax.all_to_all(fields[0], SLAB_PENCIL, split_axis=1, concat_axis=0, tiled=True),
        lax.all_to_all(fields[1], SLAB_PENCIL, split_axis=1, concat_axis=0, tiled=True),
        lax.all_to_all(fields[2], SLAB_PENCIL, split_axis=1, concat_axis=0, tiled=True),
        lax.all_to_all(fields[3], SLAB_PENCIL, split_axis=1, concat_axis=0, tiled=True),
    )
    spectra = transform_axis(
        parts[0], parts[1], row_cos, row_sin, "kx,xyz->kyz", False
    ) + transform_axis(parts[2], parts[3], row_cos, row_sin, "kx,xyz->kyz", False)
    conc_real, conc_imag, cube_real, cube_imag = spectra
    local_rows = conc_real.shape[1]
    offset = lax.axis_index(SLAB_PENCIL) * local_rows
    depth_index = jnp.arange(columns_kept, dtype=jnp.int32)
    wave_first = wavenumber(jnp.arange(NX, dtype=jnp.int32), NX)
    wave_second = wavenumber(offset + jnp.arange(local_rows, dtype=jnp.int32), NY)
    wave_third = wavenumber(depth_index, NZ)
    wave_square = (
        wave_first[:, None, None] ** 2
        + wave_second[None, :, None] ** 2
        + wave_third[None, None, :] ** 2
    )
    keep = jnp.where(depth_index == NZ // 2, 0.0, 1.0).astype(jnp.float32)[None, None, :]
    divisor = 1.0 + time_step * stiffness * wave_square * wave_square
    retain = keep * (1.0 + time_step * wave_square) / divisor
    forcing = keep * (time_step * wave_square) / divisor
    next_real = retain * conc_real - forcing * cube_real
    next_imag = retain * conc_imag - forcing * cube_imag
    back_real, back_imag = transform_axis(
        next_real, next_imag, row_cos, row_sin, "kx,xyz->kyz", True
    )
    parts = (
        lax.all_to_all(back_real, SLAB_PENCIL, split_axis=0, concat_axis=1, tiled=True),
        lax.all_to_all(back_imag, SLAB_PENCIL, split_axis=0, concat_axis=1, tiled=True),
    )
    columns = transform_axis(parts[0], parts[1], column_cos, column_sin, "ky,ayz->akz", True)
    scale = 1.0 / (NX * NY * NZ)
    partial_field = last_inverse_real(columns[0], columns[1], inverse_cos, inverse_sin) * scale
    updated = lax.all_to_all(partial_field, PENCIL, split_axis=1, concat_axis=0, tiled=True)
    mass = by_axis(jnp.sum(concentration), SLAB_PENCIL) / (NX * NY * NZ)
    return (updated, mass)


def solution(mesh):
    finer = Mesh(
        mesh.devices.reshape(mesh.shape["slab"], 4, 2, 4, 2),
        ("slab", "pencil_0", "pencil_1", "pencil_2", "pencil_3"),
    )
    in_specs = (P("slab", PENCIL, None),)
    out_specs = (P("slab", PENCIL, None), P())
    return jax.shard_map(local, mesh=finer, in_specs=in_specs, out_specs=out_specs, check_vma=False)
```

profile of v0, /device:TPU:0, one launch (start us, length us, event | category | flops | bytes accessed | tf_op | source)
XLA Modules:
  0.0 382.0 jit_solution(13667383945048793832)
XLA Ops:
  3.4 38.3 %all_to_all.156 = f32[256,8,256]{2,1,0:T(8,128)S(1)} all-to-all(f32[256,8,256]{2,1,0:T(8,128)S(1)} %get-tuple-element.3), channel_id=1, replica_groups=mesh['slab'=2,'pencil_0'=4,'pencil_1'=2,'pencil_2'=4,'pencil_3'=2] {'pen..., dimensions={0} | all-to-all | bytes 4194304 | tf_op jit(solution)/shard_map/all_to_all | solution.py:81
  41.6 5.7 %all-to-all-start = ((f32[256,8,256]{2,1,0:T(8,128)}), f32[256,8,256]{2,1,0:T(8,128)}, u32[]{:S(2)}, u32[]{:S(2)}) async-start(f32[256,8,256]{2,1,0:T(8,128)} %param.1), calls=%async_computation | async-start | bytes 4194304 | tf_op jit(solution)/shard_map/all_to_all | solution.py:80
  51.3 7.5 %fusion.52 = f32[4,128,512]{2,1,0:T(8,128)S(1)} fusion(f32[4,512,128]{2,1,0:T(8,128)S(1)} %bitcast.168), kind=kOutput, calls=%fused_computation.74 | convolution fusion | flops 1614282752 | bytes 2097152 | tf_op jit(solution)/shard_map/ky,ayz->akz/dot_general | solution.py:58
  62.2 6.5 %fusion.8 = f32[4,512,128]{1,2,0:T(8,128)S(1)} fusion(f32[4,128,512]{2,1,0:T(8,128)S(1)} %fusion.52, f32[4,512,128]{1,2,0:T(8,128)S(1)} %fusion.1), kind=kOutput, calls=%fused_computation.26 | convolution fusion | flops 1614544896 | bytes 3145728 | tf_op jit(solution)/shard_map/ky,ayz->akz/dot_general | solution.py:59
  70.0 5.8 %all-to-all-done = f32[256,8,256]{2,1,0:T(8,128)} async-done(((f32[256,8,256]{2,1,0:T(8,128)}), f32[256,8,256]{2,1,0:T(8,128)}, u32[]{:S(2)}, u32[]{:S(2)}) %all-to-all-start) | async-done | bytes 2097184 | tf_op jit(solution)/shard_map/all_to_all | solution.py:80
  75.8 7.1 %all-to-all-start.5 = ((f32[4,512,128]{2,0,1:T(4,128)}), f32[4,512,128]{2,0,1:T(4,128)S(1)}, u32[]{:S(2)}, u32[]{:S(2)}) async-start(f32[4,512,128]{2,0,1:T(4,128)} %copy.91), calls=%async_computation.5 | async-start | bytes 2097152 | tf_op jit(solution)/shard_map/all_to_all | solution.py:93
  82.9 6.3 %fusion.56 = f32[4,128,512]{2,1,0:T(8,128)S(1)} fusion(f32[4,512,128]{1,2,0:T(8,128)S(1)} %copy-done.8), kind=kOutput, calls=%fused_computation.78 | convolution fusion | flops 1614282752 | bytes 2097152 | tf_op jit(solution)/shard_map/ky,ayz->akz/dot_general | solution.py:57
  89.2 7.6 %fusion.9 = f32[4,512,128]{1,2,0:T(8,128)S(1)} fusion(f32[4,128,512]{2,1,0:T(8,128)S(1)} %fusion.56, f32[4,512,128]{2,1,0:T(8,128)S(1)} %bitcast.169), kind=kOutput, calls=%fused_computation.28 | convolution fusion | flops 1614544896 | bytes 3145728 | tf_op jit(solution)/shard_map/ky,ayz->akz/dot_general | solution.py:60
  101.6 9.1 %all-to-all-start.4 = ((f32[4,512,128]{2,0,1:T(4,128)}), f32[4,512,128]{2,0,1:T(4,128)}, u32[]{:S(2)}, u32[]{:S(2)}) async-start(f32[4,512,128]{2,0,1:T(4,128)} %copy.86), calls=%async_computation.4 | async-start | bytes 2097152 | tf_op jit(solution)/shard_map/all_to_all | solution.py:92
  122.0 5.9 %fusion.11 = f32[4,512,128]{1,2,0:T(8,128)S(1)} fusion(f32[4,128,512]{2,1,0:T(8,128)S(1)} %fusion.22, f32[16,4,8,512]{3,2,1,0:T(8,128)S(1)} %bitcast.166), kind=kOutput, calls=%fused_computation.32 | convolution fusion | flops 1614544896 | bytes 3145728 | tf_op jit(solution)/shard_map/ky,ayz->akz/dot_general | solution.py:59
  129.2 9.7 %all-to-all-start.2 = ((f32[4,512,128]{2,0,1:T(4,128)}), f32[4,512,128]{2,0,1:T(4,128)S(1)}, u32[]{:S(2)}, u32[]{:S(2)}) async-start(f32[4,512,128]{2,0,1:T(4,128)} %copy.80), calls=%async_computation.2 | async-start | bytes 2097152 | tf_op jit(solution)/shard_map/all_to_all | solution.py:91
  144.6 5.7 %fusion.12 = f32[4,512,128]{1,2,0:T(8,128)S(1)} fusion(f32[4,128,512]{2,1,0:T(8,128)S(1)} %fusion.26, f32[16,4,8,512]{3,2,1,0:T(8,128)S(1)} %bitcast.165), kind=kOutput, calls=%fused_computation.34 | convolution fusion | flops 1614544896 | bytes 3145728 | tf_op jit(solution)/shard_map/ky,ayz->akz/dot_general | solution.py:60
  151.6 6.0 %all-to-all-done.2 = f32[4,512,128]{2,0,1:T(4,128)S(1)} async-done(((f32[4,512,128]{2,0,1:T(4,128)}), f32[4,512,128]{2,0,1:T(4,128)S(1)}, u32[]{:S(2)}, u32[]{:S(2)}) %all-to-all-start.2) | async-done | bytes 1048608 | tf_op jit(solution)/shard_map/all_to_all | solution.py:91
  167.2 7.0 %fusion.46 = f32[512,4,128]{2,0,1:T(8,128)} fusion(f32[512,4,128]{2,0,1:T(8,128)S(1)} %bitcast.170), kind=kOutput, calls=%fused_computation.68 | convolution fusion | flops 1614282752 | bytes 2097152 | tf_op jit(solution)/shard_map/kx,xyz->kyz/dot_general | solution.py:58
  174.2 7.1 %fusion.48 = f32[512,4,128]{2,0,1:T(8,128)} fusion(f32[512,4,128]{2,0,1:T(8,128)S(1)} %bitcast.172), kind=kOutput, calls=%fused_computation.70 | convolution fusion | flops 1614282752 | bytes 2097152 | tf_op jit(solution)/shard_map/kx,xyz->kyz/dot_general | solution.py:58
  188.3 5.9 %fusion.59 = f32[512,4,128]{2,0,1:T(8,128)S(1)} fusion(f32[512,4,128]{2,0,1:T(8,128)S(1)} %bitcast.178), kind=kOutput, calls=%fused_computation.81 | convolution fusion | flops 1614282752 | bytes 2097152 | tf_op jit(solution)/shard_map/kx,xyz->kyz/dot_general | solution.py:57
  194.2 5.8 %fusion.5 = f32[512,4,128]{2,0,1:T(8,128)S(1)} fusion(f32[512,4,128]{2,0,1:T(8,128)S(1)} %copy-done.13, f32[512,4,128]{2,0,1:T(8,128)S(1)} %bitcast.175, f32[128]{0:T(128)S(1)} %get-tuple-element.5, f32[512,4]{0,1:T(4,128)S(1)} %broadcast_add_fusion, f32[128]{0:T(128)S(1)} %get-tuple-element.4), kind=kOutput, calls=%fused_computation.20 | convolution fusion | flops 1616117760 | bytes 3154944 | tf_op jit(solution)/shard_map/kx,xyz->kyz/dot_general | solution.py:59
  200.0 5.8 %fusion.14 = f32[512,4,128]{2,0,1:T(8,128)S(1)} fusion(f32[512,4,128]{2,0,1:T(8,128)S(1)} %fusion.5, f32[512,4,128]{2,0,1:T(8,128)S(1)} %copy-done.12, f32[512,4,128]{2,0,1:T(8,128)S(1)} %bitcast.179, f32[128]{0:T(128)S(1)} %get-tuple-element.5, f32[512,4]{0,1:T(4,128)S(1)} %broadcast_add_fusion, f32[128]{0:T(128)S(1)} %get-tuple-element.4), kind=kOutput, calls=%fused_computation.36 | convolution fusion | flops 1616642048 | bytes 4203520 | tf_op jit(solution)/shard_map/kx,xyz->kyz/dot_general | solution.py:59
  205.8 6.1 %fusion.42 = f32[512,4,128]{2,0,1:T(8,128)S(1)} fusion(f32[512,4,128]{2,0,1:T(8,128)S(1)} %fusion.14), kind=kOutput, calls=%fused_computation.64 | convolution fusion | flops 1614282752 | bytes 2097152 | tf_op jit(solution)/shard_map/kx,xyz->kyz/dot_general | solution.py:58
  211.9 5.8 %fusion.7 = f32[512,4,128]{2,0,1:T(8,128)S(1)} fusion(f32[512,4,128]{2,0,1:T(8,128)S(1)} %fusion.54, f32[512,4,128]{2,0,1:T(8,128)S(1)} %bitcast.171, f32[128]{0:T(128)S(1)} %get-tuple-element.5, f32[512,4]{0,1:T(4,128)S(1)} %broadcast_add_fusion, f32[128]{0:T(128)S(1)} %get-tuple-element.4), kind=kOutput, calls=%fused_computation.24 | convolution fusion | flops 1616117760 | bytes 3154944 | tf_op jit(solution)/shard_map/kx,xyz->kyz/dot_general | solution.py:60
  217.7 6.0 %fusion.13 = f32[512,4,128]{2,0,1:T(8,128)S(1)} fusion(f32[512,4,128]{2,0,1:T(8,128)S(1)} %fusion.7, f32[512,4,128]{2,0,1:T(8,128)S(1)} %fusion.59, f32[512,4,128]{2,0,1:T(8,128)S(1)} %bitcast.173, f32[128]{0:T(128)S(1)} %get-tuple-element.5, f32[512,4]{0,1:T(4,128)S(1)} %broadcast_add_fusion, f32[128]{0:T(128)S(1)} %get-tuple-element.4), kind=kOutput, calls=%fused_computation.35 | convolution fusion | flops 1616642048 | bytes 4203520 | tf_op jit(solution)/shard_map/kx,xyz->kyz/dot_general | solution.py:60
  223.8 5.7 %convolution_add_fusion.1 = f32[512,4,128]{2,0,1:T(8,128)S(1)} fusion(f32[512,4,128]{2,0,1:T(8,128)S(1)} %fusion.42, f32[512,4,128]{2,0,1:T(8,128)S(1)} %fusion.13), kind=kOutput, calls=%fused_computation.17 | convolution fusion | flops 1614544896 | bytes 3145728 | tf_op jit(solution)/shard_map/kx,xyz->kyz/dot_general | solution.py:59
  231.2 10.1 %all-to-all-start.7 = ((f32[512,4,128]{2,1,0:T(4,128)}), f32[512,4,128]{2,1,0:T(4,128)S(1)}, u32[]{:S(2)}, u32[]{:S(2)}) async-start(f32[512,4,128]{2,1,0:T(4,128)} %copy.97), calls=%async_computation.7 | async-start | bytes 2097152 | tf_op jit(solution)/shard_map/all_to_all | solution.py:121
  247.0 5.7 %convolution_subtract_fusion.2 = f32[512,4,128]{2,0,1:T(8,128)S(1)} fusion(f32[512,4,128]{2,0,1:T(8,128)S(1)} %fusion.50, f32[512,4,128]{2,0,1:T(8,128)S(1)} %fusion.14), kind=kOutput, calls=%fused_computation.18 | convolution fusion | flops 1614544896 | bytes 3145728 | tf_op jit(solution)/shard_map/kx,xyz->kyz/dot_general | solution.py:60
  264.5 7.5 %fusion.40 = f32[4,128,512]{2,1,0:T(8,128)S(1)} fusion(f32[4,512,128]{2,1,0:T(8,128)S(1)} %bitcast.176), kind=kOutput, calls=%fused_computation.62 | convolution fusion | flops 1614282752 | bytes 2097152 | tf_op jit(solution)/shard_map/ky,ayz->akz/dot_general | solution.py:58
  272.0 11.0 %all-to-all-done.6 = f32[512,4,128]{2,1,0:T(4,128)S(1)} async-done(((f32[512,4,128]{2,1,0:T(4,128)}), f32[512,4,128]{2,1,0:T(4,128)S(1)}, u32[]{:S(2)}, u32[]{:S(2)}) %all-to-all-start.6) | async-done | bytes 1048608 | tf_op jit(solution)/shard_map/all_to_all | solution.py:120
  283.2 7.9 %fusion.44 = f32[4,128,512]{2,1,0:T(8,128)} fusion(f32[4,512,128]{2,1,0:T(8,128)S(1)} %bitcast.180), kind=kOutput, calls=%fused_computation.66 | convolution fusion | flops 1614282752 | bytes 2097152 | tf_op jit(solution)/shard_map/ky,ayz->akz/dot_general | solution.py:57
  291.1 7.6 %fusion.3 = f32[4,512,128]{1,2,0:T(8,128)S(1)} fusion(f32[4,128,512]{2,1,0:T(8,128)S(1)} %fusion.40, f32[4,512,128]{2,1,0:T(8,128)S(1)} %bitcast.181), kind=kOutput, calls=%fused_computation.14 | convolution fusion | flops 1614544896 | bytes 3145728 | tf_op jit(solution)/shard_map/ky,ayz->akz/dot_general | solution.py:59
  299.0 9.2 %fusion.4 = f32[4,512,128]{1,2,0:T(8,128)} fusion(f32[4,128,512]{2,1,0:T(8,128)} %fusion.44, f32[4,512,128]{2,1,0:T(8,128)S(1)} %bitcast.177), kind=kOutput, calls=%fused_computation.16 | convolution fusion | flops 1614544896 | bytes 3145728 | tf_op jit(solution)/shard_map/ky,ayz->akz/dot_general | solution.py:60
  321.1 20.0 %psum.35 = f32[]{:T(128)} all-reduce(f32[]{:T(128)} %get-tuple-element.2), channel_id=1, replica_groups=mesh['slab'=2,'pencil_0'=4,'pencil_1'=2,'pencil_2'=4,'pencil_3'=2] {'slab'}, use_global_device_ids=true, to_apply=%region_1.2 | all-reduce | flops 1 | bytes 8 | tf_op jit(solution)/shard_map/psum | solution.py:22
  341.1 17.2 %psum.36 = f32[]{:T(128)} all-reduce(f32[]{:T(128)} %psum.35), channel_id=1, replica_groups=mesh['slab'=2,'pencil_0'=4,'pencil_1'=2,'pencil_2'=4,'pencil_3'=2] {'pen..., use_global_device_ids=true, to_apply=%region_2.3 | all-reduce | flops 1 | bytes 8 | tf_op jit(solution)/shard_map/psum | solution.py:22
  363.9 11.3 %psum.38 = f32[]{:T(128)} all-reduce(f32[]{:T(128)} %psum.37), channel_id=1, replica_groups=mesh['slab'=2,'pencil_0'=4,'pencil_1'=2,'pencil_2'=4,'pencil_3'=2] {'pen..., use_global_device_ids=true, to_apply=%region_4.5 | all-reduce | flops 1 | bytes 8 | tf_op jit(solution)/shard_map/psum | solution.py:22
  (78 shorter events, 95.0 us)
Async XLA Ops:
  41.6 34.1 %all-to-all-start = ((f32[256,8,256]{2,1,0:T(8,128)}), f32[256,8,256]{2,1,0:T(8,128)}, u32[]{:S(2)}, u32[]{:S(2)}) async-start(f32[256,8,256]{2,1,0:T(8,128)} %param.1), calls=%async_computation | async-start | bytes 4194304 | tf_op jit(solution)/shard_map/all_to_all | solution.py:80
  49.3 9.5 %copy-start = (f32[256,256]{1,0:T(8,128)}, f32[256,256]{1,0:T(8,128)S(1)}, u32[]{:S(2)}) copy-start(f32[256,256]{1,0:T(8,128)S(1)} %fusion.104) | copy-start | bytes 786436
  61.2 1.0 copy-start.7
  68.7 14.2 %copy-start.8 = (f32[4,512,128]{1,2,0:T(8,128)S(1)}, f32[4,512,128]{1,2,0:T(8,128)}, u32[]{:S(2)}) copy-start(f32[4,512,128]{1,2,0:T(8,128)} %copy-done.7) | copy-start | bytes 3145732
  75.8 25.8 %all-to-all-start.5 = ((f32[4,512,128]{2,0,1:T(4,128)}), f32[4,512,128]{2,0,1:T(4,128)S(1)}, u32[]{:S(2)}, u32[]{:S(2)}) async-start(f32[4,512,128]{2,0,1:T(4,128)} %copy.91), calls=%async_computation.5 | async-start | bytes 2097152 | tf_op jit(solution)/shard_map/all_to_all | solution.py:93
  101.6 27.6 %all-to-all-start.4 = ((f32[4,512,128]{2,0,1:T(4,128)}), f32[4,512,128]{2,0,1:T(4,128)}, u32[]{:S(2)}, u32[]{:S(2)}) async-start(f32[4,512,128]{2,0,1:T(4,128)} %copy.86), calls=%async_computation.4 | async-start | bytes 2097152 | tf_op jit(solution)/shard_map/all_to_all | solution.py:92
  113.0 5.7 %copy-start.3 = (f32[128,2048]{1,0:T(8,128)}, f32[128,2048]{1,0:T(8,128)S(1)}, u32[]{:S(2)}) copy-start(f32[128,2048]{1,0:T(8,128)S(1)} %convolution_negate_fusion.1) | copy-start | bytes 3145732
  113.0 5.7 %copy-start.1 = (f32[256,256]{1,0:T(8,128)S(1)}, f32[256,256]{1,0:T(8,128)}, u32[]{:S(2)}) copy-start(f32[256,256]{1,0:T(8,128)} %copy-done) | copy-start | bytes 786436
  121.0 1.0 copy-start.5
  127.9 11.0 %copy-start.6 = (f32[128,2048]{1,0:T(8,128)S(1)}, f32[128,2048]{1,0:T(8,128)}, u32[]{:S(2)}) copy-start(f32[128,2048]{1,0:T(8,128)} %copy-done.5) | copy-start | bytes 3145732
  129.2 28.4 %all-to-all-start.2 = ((f32[4,512,128]{2,0,1:T(4,128)}), f32[4,512,128]{2,0,1:T(4,128)S(1)}, u32[]{:S(2)}, u32[]{:S(2)}) async-start(f32[4,512,128]{2,0,1:T(4,128)} %copy.80), calls=%async_computation.2 | async-start | bytes 2097152 | tf_op jit(solution)/shard_map/all_to_all | solution.py:91
  138.9 5.7 %copy-start.4 = (f32[128,2048]{1,0:T(8,128)S(1)}, f32[128,2048]{1,0:T(8,128)}, u32[]{:S(2)}) copy-start(f32[128,2048]{1,0:T(8,128)} %copy-done.3) | copy-start | bytes 3145732
  157.6 23.7 %all-to-all-start.1 = ((f32[4,512,128]{2,0,1:T(4,128)}), f32[4,512,128]{2,0,1:T(4,128)S(1)}, u32[]{:S(2)}, u32[]{:S(2)}) async-start(f32[4,512,128]{2,0,1:T(4,128)} %copy.75), calls=%async_computation.1 | async-start | bytes 2097152 | tf_op jit(solution)/shard_map/all_to_all | solution.py:90
  181.3 1.2 copy-start.9
  188.2 5.9 %copy-start.13 = (f32[512,4,128]{2,0,1:T(8,128)S(1)}, f32[512,4,128]{2,0,1:T(8,128)}, u32[]{:S(2)}) copy-start(f32[512,4,128]{2,0,1:T(8,128)} %fusion.46) | copy-start | bytes 3145732
  194.2 5.8 %copy-start.12 = (f32[512,4,128]{2,0,1:T(8,128)S(1)}, f32[512,4,128]{2,0,1:T(8,128)}, u32[]{:S(2)}) copy-start(f32[512,4,128]{2,0,1:T(8,128)} %fusion.48) | copy-start | bytes 3145732
  223.8 5.8 %copy-start.10 = (f32[512,4,128]{2,0,1:T(8,128)}, f32[512,4,128]{2,0,1:T(8,128)S(1)}, u32[]{:S(2)}) copy-start(f32[512,4,128]{2,0,1:T(8,128)S(1)} %fusion.13) | copy-start | bytes 3145732
  231.2 10.1 %copy-start.11 = (f32[512,4,128]{2,0,1:T(8,128)S(1)}, f32[512,4,128]{2,0,1:T(8,128)}, u32[]{:S(2)}) copy-start(f32[512,4,128]{2,0,1:T(8,128)} %copy-done.10) | copy-start | bytes 3145732
  231.2 28.4 %all-to-all-start.7 = ((f32[512,4,128]{2,1,0:T(4,128)}), f32[512,4,128]{2,1,0:T(4,128)S(1)}, u32[]{:S(2)}, u32[]{:S(2)}) async-start(f32[512,4,128]{2,1,0:T(4,128)} %copy.97), calls=%async_computation.7 | async-start | bytes 2097152 | tf_op jit(solution)/shard_map/all_to_all | solution.py:121
  259.6 23.4 %all-to-all-start.6 = ((f32[512,4,128]{2,1,0:T(4,128)}), f32[512,4,128]{2,1,0:T(4,128)S(1)}, u32[]{:S(2)}, u32[]{:S(2)}) async-start(f32[512,4,128]{2,1,0:T(4,128)} %copy.94), calls=%async_computation.6 | async-start | bytes 2097152 | tf_op jit(solution)/shard_map/all_to_all | solution.py:120
  308.3 1.6 copy-start.2
  316.4 62.5 %all-to-all-start.8 = ((f32[4,512,256]{2,0,1:T(4,128)}), f32[4,512,256]{2,0,1:T(4,128)S(1)}, u32[]{:S(2)}, u32[]{:S(2)}) async-start(f32[4,512,256]{2,0,1:T(4,128)} %copy.104), calls=%async_computation.8 | async-start | bytes 4194304 | tf_op jit(solution)/shard_map/all_to_all | solution.py:126
where the time goes:
time: 387 us; the launch traced here: 382 us
  matrix products  168 us (43%)
  blocking collectives  95.4 us (25%)
  starting transfers between devices  56.2 us (15%)
  waiting for transfers between devices  29.5 us (8%)
  local copies, waits for them, and re-layouts  25 us (6%)
  other arithmetic  4.77 us (1%)
    psum x5, blocking collectives, by_axis(): return functools.reduce(lax.psum, axes, x)  57.1 us
    dot_general x6, matrix products, transform_axis(): jnp.einsum(form, cosines, imag_part, precision=lax.Precision.HIGHEST)  40.8 us
    dot_general x6, matrix products, transform_axis(): jnp.einsum(form, sines, imag_part, precision=lax.Precision.HIGHEST)  40 us
    all_to_all x1, blocking collectives, local(): lax.all_to_all(cube, PENCIL, split_axis=0, concat_axis=1, tiled=True)  38.3 us
    dot_general x6, matrix products, transform_axis(): jnp.einsum(form, sines, real_part, precision=lax.Precision.HIGHEST)  37.3 us
    dot_general x6, matrix products, transform_axis(): jnp.einsum(form, cosines, real_part, precision=lax.Precision.HIGHEST)  37.2 us
    all_to_all x1, waiting for transfers between devices, local(): lax.all_to_all(back_real, SLAB_PENCIL, split_axis=0, concat_axis=1, tiled...  11 us
    all_to_all x1, starting transfers between devices, local(): lax.all_to_all(back_imag, SLAB_PENCIL, split_axis=0, concat_axis=1, tiled...  10.1 us
  transfers between devices with their start and end apart: 8, of which 6 were waited for; matrix products, arithmetic and copies ran while one was open for 28% of the time, Pallas kernels for 0%

commit v1 on v0

v1 whole, which is shorter than its diff:
```python
import functools
import math

import jax
import jax.numpy as jnp
import numpy as np
from jax import lax
from jax.experimental import pallas as pl
from jax.experimental.pallas import tpu as pltpu
from jax.sharding import PartitionSpec as P

NX = 512
NY = 512
NZ = 256
KEPT = NZ // 2
DEVICES = 128
ROWS = 256
COLS = 8
HALF = ROWS // 2
TOTAL = NX * NY * NZ

time_step = 1.0
stiffness = 1.0

MESH = pl.DeviceIdType.MESH
f32 = jnp.float32
bf16 = jnp.bfloat16


def split_table(table):
    high = table.astype(np.float32).astype(bf16)
    low = (table - high.astype(np.float64)).astype(np.float32).astype(bf16)
    return np.stack([high, low])


def depth_tables():
    k = np.arange(KEPT)[:, None]
    n = np.arange(NZ)[None, :]
    angle = 2.0 * np.pi * (k * n % NZ) / NZ
    forward = np.concatenate([np.cos(angle), -np.sin(angle)], axis=0)
    weight = np.where(k == 0, 1.0, 2.0) / TOTAL
    inverse = np.stack([weight * np.cos(angle), -weight * np.sin(angle)], axis=1)
    return split_table(forward), split_table(inverse.reshape(NZ, NZ))


def plane_tables():
    c = np.arange(128)[:, None]
    b = np.arange(128)[None, :]
    out = []
    for d in range(4):
        angle = 2.0 * np.pi * (b * (4 * c + d) % 512) / 512
        cos, sin = np.cos(angle), np.sin(angle)
        out.append(np.block([[cos, sin], [-sin, cos]]))
    full = np.stack(out)
    return split_table(full), split_table(full.transpose(0, 2, 1))


def parts(value):
    high = value.astype(bf16)
    return high, (value - high.astype(f32)).astype(bf16)


def product(left, right, dims):
    dot = functools.partial(
        lax.dot_general, dimension_numbers=(dims, ((), ())), preferred_element_type=f32
    )
    return dot(left[0], right[0]) + (dot(left[0], right[1]) + dot(left[1], right[0]))


def spread(xr, xi):
    sr, si = xr[0] + xr[2], xi[0] + xi[2]
    tr, ti = xr[1] + xr[3], xi[1] + xi[3]
    pr, pi = xr[0] - xr[2], xi[0] - xi[2]
    qr, qi = xr[1] - xr[3], xi[1] - xi[3]
    return (
        (sr + tr, si + ti),
        (pr + qi, pi - qr),
        (sr - tr, si - ti),
        (pr - qi, pi + qr),
    )


def gather(vr, vi):
    sr, si = vr[0] + vr[2], vi[0] + vi[2]
    tr, ti = vr[1] + vr[3], vi[1] + vi[3]
    pr, pi = vr[0] - vr[2], vi[0] - vi[2]
    qr, qi = vr[1] - vr[3], vi[1] - vi[3]
    return (
        (sr + tr, si + ti),
        (pr - qi, pi + qr),
        (sr - tr, si - ti),
        (pr + qi, pi - qr),
    )


def shifted(me, step):
    y = (me // 64 * 2 + me // 8 % 2 + step // 64 * 2 + step // 8 % 2) % 4
    x = (me // 16 + step // 16) % 4
    z = (me // 2 + step // 2) % 4
    core = (me + step) % 2
    return y // 2 * 64 + x * 16 + y % 2 * 8 + z * 2 + core


def wave(index):
    signed = jnp.where(index < 256, index, index - 512)
    return (2.0 * math.pi / 512) * signed.astype(f32)


def kernel(
    conc_hbm, zf_hbm, zi_hbm, pf_hbm, pt_hbm,
    out_hbm, mass_ref,
    conc, zf, zi, pf, pt, send_c, send_q, plane, back, got, out, retain, forcing,
    load_sem, out_sem, local_sem, send_sem, recv_sem,
):
    slab = lax.axis_index("slab")
    pencil = lax.axis_index("pencil")
    me = slab * 64 + pencil

    barrier = pltpu.get_barrier_semaphore()

    def greet(step, carry):
        to = shifted(me, step)
        pl.semaphore_signal(
            barrier, inc=1, device_id=(to // 64, to % 64), device_id_type=MESH
        )
        return carry

    loads = [
        pltpu.make_async_copy(src, dst, load_sem.at[i])
        for i, (src, dst) in enumerate(
            [
                (conc_hbm.at[:, 0:128], conc.at[0]),
                (conc_hbm.at[:, 128:256], conc.at[1]),
                (zf_hbm, zf),
                (pf_hbm, pf),
                (pt_hbm, pt),
                (zi_hbm, zi),
            ]
        )
    ]
    for load in loads:
        load.start()
    lax.fori_loop(1, DEVICES, greet, 0)
    for load in loads:
        load.wait()

    def depth_forward(cubed, sends):
        def body(y, carry):
            value = jnp.concatenate(
                [conc[i, pl.ds(y, ROWS, stride=COLS), :] for i in range(2)], axis=1
            )
            if cubed:
                value = value * value * value
            result = product((zf[0], zf[1]), parts(value), ((1,), (1,)))
            for i in range(2):
                for h in range(2):
                    sends[h, pl.ds(i * COLS + y, KEPT, stride=2 * COLS), :] = result[
                        i * KEPT : (i + 1) * KEPT, h * HALF : (h + 1) * HALF
                    ]
            return carry

        lax.fori_loop(0, COLS, body, 0)

    def forward_block(sends, field, h, to):
        return (
            sends.at[h, pl.ds(pl.multiple_of(to * 16, 16), 16), :].reshape(2, 8, 128),
            plane.at[
                2 * field : 2 * field + 2,
                pl.ds(pl.multiple_of(pencil * COLS, COLS), COLS),
                pl.ds(pl.multiple_of(slab * ROWS + h * HALF, HALF), HALF),
            ],
        )

    def backward_block(h, to):
        return (
            back.at[
                :,
                pl.ds(pl.multiple_of(to % 64 * COLS, COLS), COLS),
                pl.ds(pl.multiple_of(to // 64 * ROWS + h * HALF, HALF), HALF),
            ],
            got.at[h, pl.ds(pl.multiple_of(me * 16, 16), 16), :].reshape(2, 8, 128),
        )

    def exchange(block, stage):
        src, dst = block(me)
        pltpu.make_async_copy(src, dst, local_sem.at[stage]).start()

        def send(turn, carry):
            to = shifted(me, turn * 21 % 128)
            src, dst = block(to)
            pltpu.make_async_remote_copy(
                src_ref=src,
                dst_ref=dst,
                send_sem=send_sem.at[stage],
                recv_sem=recv_sem.at[stage],
                device_id=(to // 64, to % 64),
                device_id_type=MESH,
            ).start()
            return carry

        lax.fori_loop(1, DEVICES, send, 0)

    def arrived(block, stage):
        src, dst = block(me)
        pltpu.make_async_copy(src, dst, local_sem.at[stage]).wait()
        rows = pl.ds(0, 16 * (DEVICES - 1))
        everything = pltpu.make_async_remote_copy(
            src_ref=got.at[0, rows, :],
            dst_ref=got.at[0, rows, :],
            send_sem=send_sem.at[stage],
            recv_sem=recv_sem.at[stage],
            device_id=(slab, pencil),
            device_id_type=MESH,
        )
        everything.wait()

    def second_forward(field):
        def body(i, carry):
            lanes = pl.ds(pl.multiple_of(i * 256, 256), 256)
            xr = [plane[2 * field, a * 128 : (a + 1) * 128, lanes] for a in range(4)]
            xi = [plane[2 * field + 1, a * 128 : (a + 1) * 128, lanes] for a in range(4)]
            for d, (ur, ui) in enumerate(spread(xr, xi)):
                result = product(
                    (pf[0, d], pf[1, d]), parts(jnp.concatenate([ur, ui], axis=0)), ((1,), (0,))
                )
                plane[2 * field, d * 128 : (d + 1) * 128, lanes] = result[:128]
                plane[2 * field + 1, d * 128 : (d + 1) * 128, lanes] = result[128:]
            return carry

        lax.fori_loop(0, 2, body, 0)

    def first_forward(field, rows):
        xr = [plane[2 * field, rows, a * 128 : (a + 1) * 128] for a in range(4)]
        xi = [plane[2 * field + 1, rows, a * 128 : (a + 1) * 128] for a in range(4)]
        return [
            product(parts(jnp.concatenate([ur, ui], axis=1)), (pt[0, d], pt[1, d]), ((1,), (0,)))
            for d, (ur, ui) in enumerate(spread(xr, xi))
        ]

    def row_block(i):
        return pl.ds(pl.multiple_of(i * 128, 128), 128)

    def first_forward_conc():
        def body(i, carry):
            rows = row_block(i)
            for d, result in enumerate(first_forward(0, rows)):
                plane[0, rows, d * 128 : (d + 1) * 128] = result[:, :128]
                plane[1, rows, d * 128 : (d + 1) * 128] = result[:, 128:]
            return carry

        lax.fori_loop(0, 4, body, 0)

    def multipliers():
        third = wave(me) * (512 // NZ)

        def body(i, carry):
            rows = row_block(i)
            row = lax.broadcasted_iota(jnp.int32, (128, 512), 0)
            lane = lax.broadcasted_iota(jnp.int32, (128, 512), 1)
            second = wave(row * 4 + i)
            first = wave(lane % 128 * 4 + lane // 128)
            square = first * first + second * second + third * third
            divisor = 1.0 + time_step * stiffness * square * square
            retain[rows, :] = (1.0 + time_step * square) / divisor
            forcing[rows, :] = (time_step * square) / divisor
            return carry

        lax.fori_loop(0, 4, body, 0)

    def combine_and_first_inverse():
        def body(i, carry):
            rows = row_block(i)
            vr, vi = [], []
            for d, cube in enumerate(first_forward(1, rows)):
                lanes = slice(d * 128, (d + 1) * 128)
                keep, force = retain[rows, lanes], forcing[rows, lanes]
                next_real = keep * plane[0, rows, lanes] - force * cube[:, :128]
                next_imag = keep * plane[1, rows, lanes] - force * cube[:, 128:]
                result = product(
                    parts(jnp.concatenate([next_real, next_imag], axis=1)),
                    (pf[0, d], pf[1, d]),
                    ((1,), (0,)),
                )
                vr.append(result[:, :128])
                vi.append(result[:, 128:])
            for a, (xr, xi) in enumerate(gather(vr, vi)):
                plane[2, rows, a * 128 : (a + 1) * 128] = xr
                plane[3, rows, a * 128 : (a + 1) * 128] = xi
            return carry

        lax.fori_loop(0, 4, body, 0)

    def second_inverse(h, mass):
        def body(i, carry):
            lanes = pl.ds(pl.multiple_of(i * ROWS + h * HALF, HALF), HALF)
            vr, vi = [], []
            for d in range(4):
                block = slice(d * 128, (d + 1) * 128)
                result = product(
                    (pt[0, d], pt[1, d]),
                    parts(jnp.concatenate([plane[2, block, lanes], plane[3, block, lanes]], axis=0)),
                    ((1,), (0,)),
                )
                vr.append(result[:128])
                vi.append(result[128:])
            for a, (xr, xi) in enumerate(gather(vr, vi)):
                block = slice(a * 128, (a + 1) * 128)
                back[0, block, lanes] = xr
                back[1, block, lanes] = jnp.where(me == 0, mass, xi)
            return carry

        lax.fori_loop(0, 2, body, 0)

    def depth_inverse(h):
        def body(y, carry):
            value = got[h, pl.ds(y, NZ, stride=COLS), :]
            result = product(parts(value), (zi[0], zi[1]), ((0,), (0,)))
            for i in range(2):
                out[i, pl.ds(h * HALF * COLS + y, HALF, stride=COLS), :] = result[
                    :, i * 128 : (i + 1) * 128
                ]
            return carry

        lax.fori_loop(0, COLS, body, 0)

    depth_forward(False, send_c)
    pl.semaphore_wait(barrier, DEVICES - 1)
    for h in range(2):
        exchange(functools.partial(forward_block, send_c, 0, h), h)
    depth_forward(True, send_q)
    for h in range(2):
        exchange(functools.partial(forward_block, send_q, 1, h), 2 + h)
    multipliers()
    for h in range(2):
        arrived(functools.partial(forward_block, send_c, 0, h), h)
    second_forward(0)
    first_forward_conc()
    mass = jnp.broadcast_to(plane[0, 0:1, 0:1], (128, 128)) * (1.0 / TOTAL)
    for h in range(2):
        arrived(functools.partial(forward_block, send_q, 1, h), 2 + h)
    second_forward(1)
    combine_and_first_inverse()
    for h in range(2):
        second_inverse(h, mass)
        exchange(functools.partial(backward_block, h), 4 + h)
    outs = []
    for h in range(2):
        arrived(functools.partial(backward_block, h), 4 + h)
        depth_inverse(h)
        rows = pl.ds(h * HALF * COLS, HALF * COLS)
        for i in range(2):
            outs.append(
                pltpu.make_async_copy(
                    out.at[i, rows, :],
                    out_hbm.at[rows, i * 128 : (i + 1) * 128],
                    out_sem.at[h, i],
                )
            )
            outs[-1].start()
    mass_ref[...] = got[0, 8:16, :]
    for copy in outs:
        copy.wait()


def local(concentration):
    zf, zi = depth_tables()
    pf, pt = plane_tables()
    anywhere = pl.BlockSpec(memory_space=pl.ANY)
    updated, mass = pl.pallas_call(
        kernel,
        out_shape=(
            jax.ShapeDtypeStruct((ROWS * COLS, NZ), f32),
            jax.ShapeDtypeStruct((8, 128), f32),
        ),
        in_specs=[anywhere] * 5,
        out_specs=(anywhere, pl.BlockSpec(memory_space=pltpu.VMEM)),
        scratch_shapes=[
            pltpu.VMEM((2, ROWS * COLS, 128), f32),
            pltpu.VMEM(zf.shape, bf16),
            pltpu.VMEM(zi.shape, bf16),
            pltpu.VMEM(pf.shape, bf16),
            pltpu.VMEM(pt.shape, bf16),
            pltpu.VMEM((2, KEPT * 16, HALF), f32),
            pltpu.VMEM((2, KEPT * 16, HALF), f32),
            pltpu.VMEM((4, NY, NX), f32),
            pltpu.VMEM((2, NY, NX), f32),
            pltpu.VMEM((2, KEPT * 16, HALF), f32),
            pltpu.VMEM((2, ROWS * COLS, 128), f32),
            pltpu.VMEM((NY, NX), f32),
            pltpu.VMEM((NY, NX), f32),
            pltpu.SemaphoreType.DMA((6,)),
            pltpu.SemaphoreType.DMA((2, 2)),
            pltpu.SemaphoreType.DMA((6,)),
            pltpu.SemaphoreType.DMA((6,)),
            pltpu.SemaphoreType.DMA((6,)),
        ],
        compiler_params=pltpu.CompilerParams(
            collective_id=0, has_side_effects=True, vmem_limit_bytes=56 * 2**20
        ),
        name="cahn_hilliard_step",
    )(
        concentration.reshape(ROWS * COLS, NZ),
        jnp.asarray(zf), jnp.asarray(zi), jnp.asarray(pf), jnp.asarray(pt),
    )
    return updated.reshape(ROWS, COLS, NZ), mass[0, 0]


def solution(mesh):
    return jax.shard_map(
        local,
        mesh=mesh,
        in_specs=(P("slab", "pencil", None),),
        out_specs=(P("slab", "pencil", None), P()),
        check_vma=False,
    )
```

time: 387 us -> 107 us (0.28); the launches traced: 382 us -> 107 us
  matrix products: 168 us -> 0 us
  Pallas kernels: 0 us -> 102 us
  blocking collectives: 95.4 us -> 0 us
  starting transfers between devices: 56.2 us -> 0 us
  waiting for transfers between devices: 29.5 us -> 0 us
  local copies, waits for them, and re-layouts: 25 us -> 4.23 us
  other arithmetic: 4.77 us -> 0 us
    dot_general x30 -> x0, matrix products: 168 us -> none  [the longest x6 40.8 us: transform_axis(): jnp.einsum(form, cosines, imag_part, precision=lax.Precision.HIGHEST)]
    pallas_call x0 -> x1, Pallas kernels: none -> 102 us  [local(): pl.pallas_call(kernel, out_shape=(jax.ShapeDtypeStruct((ROWS * COLS, NZ),...]
    psum x5 -> x0, blocking collectives: 57.1 us -> none  [by_axis(): return functools.reduce(lax.psum, axes, x)]
    all_to_all x8 -> x0, starting transfers between devices: 56.2 us -> none  [the longest x1 10.1 us: local(): lax.all_to_all(back_imag, SLAB_PENCIL, split_axis=0, concat_axis=1, tiled...]
    all_to_all x1 -> x0, blocking collectives: 38.3 us -> none  [local(): lax.all_to_all(cube, PENCIL, split_axis=0, concat_axis=1, tiled=True)]
    all_to_all x8 -> x0, waiting for transfers between devices: 29.5 us -> none  [the longest x1 11 us: local(): lax.all_to_all(back_real, SLAB_PENCIL, split_axis=0, concat_axis=1, tiled...]
    all_to_all x13 -> x0, local copies, waits for them, and re-layouts: 9.26 us -> none  [the longest x2 2.94 us: local(): lax.all_to_all(fields[2], SLAB_PENCIL, split_axis=1, concat_axis=0, tiled...]
    sub x4 -> x0, local copies, waits for them, and re-layouts: 6.02 us -> none  [the longest x2 3.41 us: transform_axis(): return (cos_real - sin_imag, cos_imag + sin_real)]
  transfers between devices with their start and end apart: 8 -> 0, of which waited for: 6 -> 0; matrix products, arithmetic and copies ran while one was open for 28% -> 0% of each run, Pallas kernels for 0% -> 0%
where the time goes in v1:
time: 107 us
  Pallas kernels  102 us (95%)
  local copies, waits for them, and re-layouts  4.23 us (4%)
    pallas_call x1, Pallas kernels, local(): pl.pallas_call(kernel, out_shape=(jax.ShapeDtypeStruct((ROWS * COLS, NZ),...  102 us
    unnamed x1, local copies, waits for them, and re-layouts  3.04 us

profile of v1, /device:TPU:0, one launch (start us, length us, event | category | flops | bytes accessed | tf_op | source)
XLA Modules:
  0.0 106.9 jit_solution(8433999258088509901)
XLA Ops:
  0.6 102.1 %cahn_hilliard_step.1 = (f32[2048,256]{1,0:T(8,128)}, f32[8,128]{1,0:T(8,128)}) custom-call(f32[2048,256]{1,0:T(8,128)} %bitcast.3, bf16[2,256,256]{2,1,0:T(8,128)(2,1)} %constant.8.clone.zf_hbm, bf16[2,256,256]{2,1,0:T(8,128)(2,1)} %constant.9.clone.zi_hbm, bf16[2,4,256,256]{3,2,1,0:T(8,128)(2,1)} %constant.10.clone.pf_hbm, ...), custom_call_target="tpu_custom_call" | custom-call | tf_op jit(solution)/shard_map/cahn_hilliard_step/pallas_call | solution.py:369
  102.7 1.2 %slice.3 = f32[1,1]{1,0:T(1,128)} slice(f32[8,128]{1,0:T(8,128)} %get-tuple-element.5), slice={[0:1], [0:1]} | slice | bytes 8 | tf_op jit(solution)/shard_map/slice | solution.py:405
  103.9 3.0 %copy.8 = f32[256,8,256]{2,1,0:T(8,128)} copy(f32[256,8,256]{2,1,0:T(8,128)} %bitcast.4) | data formatting | bytes 4194304

commit v2 on v1

--- a/solution.py
+++ b/solution.py
@@ -93,14 +93,6 @@
     )
 
 
-def shifted(me, step):
-    y = (me // 64 * 2 + me // 8 % 2 + step // 64 * 2 + step // 8 % 2) % 4
-    x = (me // 16 + step // 16) % 4
-    z = (me // 2 + step // 2) % 4
-    core = (me + step) % 2
-    return y // 2 * 64 + x * 16 + y % 2 * 8 + z * 2 + core
-
-
 def wave(index):
     signed = jnp.where(index < 256, index, index - 512)
     return (2.0 * math.pi / 512) * signed.astype(f32)
@@ -119,9 +111,12 @@
     barrier = pltpu.get_barrier_semaphore()
 
     def greet(step, carry):
-        to = shifted(me, step)
+        to = lax.rem(me + step, DEVICES)
         pl.semaphore_signal(
-            barrier, inc=1, device_id=(to // 64, to % 64), device_id_type=MESH
+            barrier,
+            inc=1,
+            device_id=(lax.div(to, 64), lax.rem(to, 64)),
+            device_id_type=MESH,
         )
         return carry
 
@@ -144,26 +139,38 @@
     for load in loads:
         load.wait()
 
-    def depth_forward(cubed, sends):
-        def body(y, carry):
+    def depth_forward(cubed, sends, h):
+        def body(j, carry):
             value = jnp.concatenate(
-                [conc[i, pl.ds(y, ROWS, stride=COLS), :] for i in range(2)], axis=1
+                [
+                    jnp.concatenate(
+                        [
+                            conc[i, pl.ds(h * HALF * COLS + 2 * j + e, HALF, stride=COLS), :]
+                            for i in range(2)
+                        ],
+                        axis=1,
+                    )
+                    for e in range(2)
+                ],
+                axis=0,
             )
             if cubed:
                 value = value * value * value
             result = product((zf[0], zf[1]), parts(value), ((1,), (1,)))
             for i in range(2):
-                for h in range(2):
-                    sends[h, pl.ds(i * COLS + y, KEPT, stride=2 * COLS), :] = result[
-                        i * KEPT : (i + 1) * KEPT, h * HALF : (h + 1) * HALF
+                for e in range(2):
+                    sends[h, pl.ds(i * COLS + 2 * j + e, KEPT, stride=2 * COLS), :] = result[
+                        i * KEPT : (i + 1) * KEPT, e * HALF : (e + 1) * HALF
                     ]
             return carry
 
-        lax.fori_loop(0, COLS, body, 0)
-
-    def forward_block(sends, field, h, to):
+        lax.fori_loop(0, COLS // 2, body, 0)
+
+    def forward_block(sends, field, h, to_slab, to_pencil):
         return (
-            sends.at[h, pl.ds(pl.multiple_of(to * 16, 16), 16), :].reshape(2, 8, 128),
+            sends.at[
+                h, pl.ds(pl.multiple_of(to_slab * 1024 + to_pencil * 16, 16), 16), :
+            ].reshape(2, 8, 128),
             plane.at[
                 2 * field : 2 * field + 2,
                 pl.ds(pl.multiple_of(pencil * COLS, COLS), COLS),
@@ -171,37 +178,42 @@
             ],
         )
 
-    def backward_block(h, to):
+    def backward_block(h, to_slab, to_pencil):
         return (
             back.at[
                 :,
-                pl.ds(pl.multiple_of(to % 64 * COLS, COLS), COLS),
-                pl.ds(pl.multiple_of(to // 64 * ROWS + h * HALF, HALF), HALF),
+                pl.ds(pl.multiple_of(to_pencil * COLS, COLS), COLS),
+                pl.ds(pl.multiple_of(to_slab * ROWS + h * HALF, HALF), HALF),
             ],
             got.at[h, pl.ds(pl.multiple_of(me * 16, 16), 16), :].reshape(2, 8, 128),
         )
 
     def exchange(block, stage):
-        src, dst = block(me)
+        src, dst = block(slab, pencil)
         pltpu.make_async_copy(src, dst, local_sem.at[stage]).start()
 
-        def send(turn, carry):
-            to = shifted(me, turn * 21 % 128)
-            src, dst = block(to)
+        def send(to_slab, to_pencil):
+            src, dst = block(to_slab, to_pencil)
             pltpu.make_async_remote_copy(
                 src_ref=src,
                 dst_ref=dst,
                 send_sem=send_sem.at[stage],
                 recv_sem=recv_sem.at[stage],
-                device_id=(to // 64, to % 64),
+                device_id=(to_slab, to_pencil),
                 device_id_type=MESH,
             ).start()
-            return carry
-
-        lax.fori_loop(1, DEVICES, send, 0)
+
+        def pair(turn, carry):
+            to_pencil = lax.rem(pencil + 11 * turn, 64)
+            send(slab, to_pencil)
+            send(1 - slab, to_pencil)
+            return carry
+
+        send(1 - slab, pencil)
+        lax.fori_loop(1, 64, pair, 0)
 
     def arrived(block, stage):
-        src, dst = block(me)
+        src, dst = block(slab, pencil)
         pltpu.make_async_copy(src, dst, local_sem.at[stage]).wait()
         rows = pl.ds(0, 16 * (DEVICES - 1))
         everything = pltpu.make_async_remote_copy(
@@ -214,20 +226,24 @@
         )
         everything.wait()
 
-    def second_forward(field):
-        def body(i, carry):
-            lanes = pl.ds(pl.multiple_of(i * 256, 256), 256)
-            xr = [plane[2 * field, a * 128 : (a + 1) * 128, lanes] for a in range(4)]
-            xi = [plane[2 * field + 1, a * 128 : (a + 1) * 128, lanes] for a in range(4)]
-            for d, (ur, ui) in enumerate(spread(xr, xi)):
-                result = product(
-                    (pf[0, d], pf[1, d]), parts(jnp.concatenate([ur, ui], axis=0)), ((1,), (0,))
-                )
-                plane[2 * field, d * 128 : (d + 1) * 128, lanes] = result[:128]
-                plane[2 * field + 1, d * 128 : (d + 1) * 128, lanes] = result[128:]
-            return carry
-
-        lax.fori_loop(0, 2, body, 0)
+    def lane_halves(h):
+        return [slice(i * ROWS + h * HALF, i * ROWS + (h + 1) * HALF) for i in range(2)]
+
+    def both(index, rows, h):
+        return jnp.concatenate([plane[index, rows, lanes] for lanes in lane_halves(h)], axis=1)
+
+    def second_forward(field, h):
+        quarters = [slice(a * 128, (a + 1) * 128) for a in range(4)]
+        xr = [both(2 * field, rows, h) for rows in quarters]
+        xi = [both(2 * field + 1, rows, h) for rows in quarters]
+        for d, (ur, ui) in enumerate(spread(xr, xi)):
+            result = product(
+                (pf[0, d], pf[1, d]), parts(jnp.concatenate([ur, ui], axis=0)), ((1,), (0,))
+            )
+            for i, lanes in enumerate(lane_halves(h)):
+                half = slice(i * HALF, (i + 1) * HALF)
+                plane[2 * field, quarters[d], lanes] = result[:128, half]
+                plane[2 * field + 1, quarters[d], lanes] = result[128:, half]
 
     def first_forward(field, rows):
         xr = [plane[2 * field, rows, a * 128 : (a + 1) * 128] for a in range(4)]
@@ -291,54 +307,52 @@
         lax.fori_loop(0, 4, body, 0)
 
     def second_inverse(h, mass):
-        def body(i, carry):
-            lanes = pl.ds(pl.multiple_of(i * ROWS + h * HALF, HALF), HALF)
-            vr, vi = [], []
-            for d in range(4):
-                block = slice(d * 128, (d + 1) * 128)
-                result = product(
-                    (pt[0, d], pt[1, d]),
-                    parts(jnp.concatenate([plane[2, block, lanes], plane[3, block, lanes]], axis=0)),
-                    ((1,), (0,)),
-                )
-                vr.append(result[:128])
-                vi.append(result[128:])
-            for a, (xr, xi) in enumerate(gather(vr, vi)):
-                block = slice(a * 128, (a + 1) * 128)
-                back[0, block, lanes] = xr
-                back[1, block, lanes] = jnp.where(me == 0, mass, xi)
-            return carry
-
-        lax.fori_loop(0, 2, body, 0)
+        quarters = [slice(a * 128, (a + 1) * 128) for a in range(4)]
+        vr, vi = [], []
+        for d in range(4):
+            value = jnp.concatenate([both(2, quarters[d], h), both(3, quarters[d], h)], axis=0)
+            result = product((pt[0, d], pt[1, d]), parts(value), ((1,), (0,)))
+            vr.append(result[:128])
+            vi.append(result[128:])
+        for a, (xr, xi) in enumerate(gather(vr, vi)):
+            xi = jnp.where(me == 0, mass, xi)
+            for i, lanes in enumerate(lane_halves(h)):
+                half = slice(i * HALF, (i + 1) * HALF)
+                back[0, quarters[a], lanes] = xr[:, half]
+                back[1, quarters[a], lanes] = xi[:, half]
 
     def depth_inverse(h):
-        def body(y, carry):
-            value = got[h, pl.ds(y, NZ, stride=COLS), :]
+        def body(j, carry):
+            value = jnp.concatenate(
+                [got[h, pl.ds(2 * j + e, NZ, stride=COLS), :] for e in range(2)], axis=1
+            )
             result = product(parts(value), (zi[0], zi[1]), ((0,), (0,)))
-            for i in range(2):
-                out[i, pl.ds(h * HALF * COLS + y, HALF, stride=COLS), :] = result[
-                    :, i * 128 : (i + 1) * 128
-                ]
-            return carry
-
-        lax.fori_loop(0, COLS, body, 0)
-
-    depth_forward(False, send_c)
+            for e in range(2):
+                for i in range(2):
+                    out[i, pl.ds(h * HALF * COLS + 2 * j + e, HALF, stride=COLS), :] = result[
+                        e * HALF : (e + 1) * HALF, i * 128 : (i + 1) * 128
+                    ]
+            return carry
+
+        lax.fori_loop(0, COLS // 2, body, 0)
+
+    depth_forward(False, send_c, 0)
     pl.semaphore_wait(barrier, DEVICES - 1)
+    exchange(functools.partial(forward_block, send_c, 0, 0), 0)
+    depth_forward(False, send_c, 1)
+    exchange(functools.partial(forward_block, send_c, 0, 1), 1)
     for h in range(2):
-        exchange(functools.partial(forward_block, send_c, 0, h), h)
-    depth_forward(True, send_q)
-    for h in range(2):
+        depth_forward(True, send_q, h)
         exchange(functools.partial(forward_block, send_q, 1, h), 2 + h)
     multipliers()
     for h in range(2):
         arrived(functools.partial(forward_block, send_c, 0, h), h)
-    second_forward(0)
+        second_forward(0, h)
     first_forward_conc()
-    mass = jnp.broadcast_to(plane[0, 0:1, 0:1], (128, 128)) * (1.0 / TOTAL)
+    mass = jnp.broadcast_to(plane[0, 0:1, 0:1], (128, 256)) * (1.0 / TOTAL)
     for h in range(2):
         arrived(functools.partial(forward_block, send_q, 1, h), 2 + h)
-    second_forward(1)
+        second_forward(1, h)
     combine_and_first_inverse()
     for h in range(2):
         second_inverse(h, mass)

time: 107 us -> 99.3 us (0.928)
  Pallas kernels: 102 us -> 93.8 us
    pallas_call x1, Pallas kernels: 102 us -> 93.8 us  [local(): pl.pallas_call(kernel, out_shape=(jax.ShapeDtypeStruct((ROWS * COLS, NZ),...]
where the time goes in v2:
time: 99.3 us; the launch traced here: 98.7 us
  Pallas kernels  93.8 us (94%)
  local copies, waits for them, and re-layouts  4.23 us (4%)
    pallas_call x1, Pallas kernels, local(): pl.pallas_call(kernel, out_shape=(jax.ShapeDtypeStruct((ROWS * COLS, NZ),...  93.8 us
    unnamed x1, local copies, waits for them, and re-layouts  3.04 us

profile of v2, /device:TPU:0, one launch (start us, length us, event | category | flops | bytes accessed | tf_op | source)
XLA Modules:
  0.0 98.7 jit_solution(9932424357893423472)
XLA Ops:
  0.6 93.8 %cahn_hilliard_step.1 = (f32[2048,256]{1,0:T(8,128)}, f32[8,128]{1,0:T(8,128)}) custom-call(f32[2048,256]{1,0:T(8,128)} %bitcast.3, bf16[2,256,256]{2,1,0:T(8,128)(2,1)} %constant.8.clone.zf_hbm, bf16[2,256,256]{2,1,0:T(8,128)(2,1)} %constant.9.clone.zi_hbm, bf16[2,4,256,256]{3,2,1,0:T(8,128)(2,1)} %constant.10.clone.pf_hbm, ...), custom_call_target="tpu_custom_call" | custom-call | tf_op jit(solution)/shard_map/cahn_hilliard_step/pallas_call | solution.py:383
  94.5 1.2 %slice.3 = f32[1,1]{1,0:T(1,128)} slice(f32[8,128]{1,0:T(8,128)} %get-tuple-element.5), slice={[0:1], [0:1]} | slice | bytes 8 | tf_op jit(solution)/shard_map/slice | solution.py:419
  95.7 3.0 %copy.8 = f32[256,8,256]{2,1,0:T(8,128)} copy(f32[256,8,256]{2,1,0:T(8,128)} %bitcast.4) | data formatting | bytes 4194304

commit v3 on v2

--- a/solution.py
+++ b/solution.py
@@ -18,6 +18,7 @@
 COLS = 8
 HALF = ROWS // 2
 TOTAL = NX * NY * NZ
+FIRST = 1
 
 time_step = 1.0
 stiffness = 1.0
@@ -27,10 +28,11 @@
 bf16 = jnp.bfloat16
 
 
-def split_table(table):
-    high = table.astype(np.float32).astype(bf16)
-    low = (table - high.astype(np.float64)).astype(np.float32).astype(bf16)
-    return np.stack([high, low])
+def all_tables():
+    full = np.concatenate([depth_tables(), *plane_tables()])
+    high = full.astype(np.float32).astype(bf16)
+    low = (full - high.astype(np.float64)).astype(np.float32).astype(bf16)
+    return np.stack([high, low], axis=1).reshape(20, 256, 256)
 
 
 def depth_tables():
@@ -40,7 +42,7 @@
     forward = np.concatenate([np.cos(angle), -np.sin(angle)], axis=0)
     weight = np.where(k == 0, 1.0, 2.0) / TOTAL
     inverse = np.stack([weight * np.cos(angle), -weight * np.sin(angle)], axis=1)
-    return split_table(forward), split_table(inverse.reshape(NZ, NZ))
+    return forward, inverse.reshape(NZ, NZ)
 
 
 def plane_tables():
@@ -52,7 +54,7 @@
         cos, sin = np.cos(angle), np.sin(angle)
         out.append(np.block([[cos, sin], [-sin, cos]]))
     full = np.stack(out)
-    return split_table(full), split_table(full.transpose(0, 2, 1))
+    return full, full.transpose(0, 2, 1)
 
 
 def parts(value):
@@ -99,10 +101,10 @@
 
 
 def kernel(
-    conc_hbm, zf_hbm, zi_hbm, pf_hbm, pt_hbm,
-    out_hbm, mass_ref,
-    conc, zf, zi, pf, pt, send_c, send_q, plane, back, got, out, retain, forcing,
-    load_sem, out_sem, local_sem, send_sem, recv_sem,
+    conc_hbm, tables_hbm,
+    out, mass_ref,
+    conc, tables, send_c, send_q, plane, back, got, retain, forcing,
+    load_sem, local_sem, send_sem, recv_sem,
 ):
     slab = lax.axis_index("slab")
     pencil = lax.axis_index("pencil")
@@ -126,18 +128,25 @@
             [
                 (conc_hbm.at[:, 0:128], conc.at[0]),
                 (conc_hbm.at[:, 128:256], conc.at[1]),
-                (zf_hbm, zf),
-                (pf_hbm, pf),
-                (pt_hbm, pt),
-                (zi_hbm, zi),
+                (tables_hbm.at[0:2], tables.at[0:2]),
+                (tables_hbm.at[2:20], tables.at[2:20]),
             ]
         )
     ]
     for load in loads:
         load.start()
     lax.fori_loop(1, DEVICES, greet, 0)
-    for load in loads:
+    for load in loads[:3]:
         load.wait()
+
+    def table(first):
+        return tables[first], tables[first + 1]
+
+    def forward_table(d):
+        return table(4 + 2 * d)
+
+    def turned_table(d):
+        return table(12 + 2 * d)
 
     def depth_forward(cubed, sends, h):
         def body(j, carry):
@@ -156,7 +165,7 @@
             )
             if cubed:
                 value = value * value * value
-            result = product((zf[0], zf[1]), parts(value), ((1,), (1,)))
+            result = product(table(0), parts(value), ((1,), (1,)))
             for i in range(2):
                 for e in range(2):
                     sends[h, pl.ds(i * COLS + 2 * j + e, KEPT, stride=2 * COLS), :] = result[
@@ -188,10 +197,11 @@
             got.at[h, pl.ds(pl.multiple_of(me * 16, 16), 16), :].reshape(2, 8, 128),
         )
 
-    def exchange(block, stage):
+    def keep_own(block, stage):
         src, dst = block(slab, pencil)
         pltpu.make_async_copy(src, dst, local_sem.at[stage]).start()
 
+    def exchange(block, stage, core):
         def send(to_slab, to_pencil):
             src, dst = block(to_slab, to_pencil)
             pltpu.make_async_remote_copy(
@@ -203,14 +213,20 @@
                 device_id_type=MESH,
             ).start()
 
+        chip = lax.div(pencil, 2)
+
         def pair(turn, carry):
-            to_pencil = lax.rem(pencil + 11 * turn, 64)
+            to_pencil = 2 * lax.rem(chip + 11 * turn, 32) + core
             send(slab, to_pencil)
             send(1 - slab, to_pencil)
             return carry
 
-        send(1 - slab, pencil)
-        lax.fori_loop(1, 64, pair, 0)
+        lax.fori_loop(1, 32, pair, 0)
+        send(1 - slab, 2 * chip + core)
+
+        @pl.when(lax.rem(pencil, 2) != core)
+        def _():
+            send(slab, 2 * chip + core)
 
     def arrived(block, stage):
         src, dst = block(slab, pencil)
@@ -238,7 +254,7 @@
         xi = [both(2 * field + 1, rows, h) for rows in quarters]
         for d, (ur, ui) in enumerate(spread(xr, xi)):
             result = product(
-                (pf[0, d], pf[1, d]), parts(jnp.concatenate([ur, ui], axis=0)), ((1,), (0,))
+                forward_table(d), parts(jnp.concatenate([ur, ui], axis=0)), ((1,), (0,))
             )
             for i, lanes in enumerate(lane_halves(h)):
                 half = slice(i * HALF, (i + 1) * HALF)
@@ -249,7 +265,7 @@
         xr = [plane[2 * field, rows, a * 128 : (a + 1) * 128] for a in range(4)]
         xi = [plane[2 * field + 1, rows, a * 128 : (a + 1) * 128] for a in range(4)]
         return [
-            product(parts(jnp.concatenate([ur, ui], axis=1)), (pt[0, d], pt[1, d]), ((1,), (0,)))
+            product(parts(jnp.concatenate([ur, ui], axis=1)), turned_table(d), ((1,), (0,)))
             for d, (ur, ui) in enumerate(spread(xr, xi))
         ]
 
@@ -294,7 +310,7 @@
                 next_imag = keep * plane[1, rows, lanes] - force * cube[:, 128:]
                 result = product(
                     parts(jnp.concatenate([next_real, next_imag], axis=1)),
-                    (pf[0, d], pf[1, d]),
+                    forward_table(d),
                     ((1,), (0,)),
                 )
                 vr.append(result[:, :128])
@@ -311,7 +327,7 @@
         vr, vi = [], []
         for d in range(4):
             value = jnp.concatenate([both(2, quarters[d], h), both(3, quarters[d], h)], axis=0)
-            result = product((pt[0, d], pt[1, d]), parts(value), ((1,), (0,)))
+            result = product(turned_table(d), parts(value), ((1,), (0,)))
             vr.append(result[:128])
             vi.append(result[128:])
         for a, (xr, xi) in enumerate(gather(vr, vi)):
@@ -326,7 +342,7 @@
             value = jnp.concatenate(
                 [got[h, pl.ds(2 * j + e, NZ, stride=COLS), :] for e in range(2)], axis=1
             )
-            result = product(parts(value), (zi[0], zi[1]), ((0,), (0,)))
+            result = product(parts(value), table(2), ((0,), (0,)))
             for e in range(2):
                 for i in range(2):
                     out[i, pl.ds(h * HALF * COLS + 2 * j + e, HALF, stride=COLS), :] = result[
@@ -336,87 +352,103 @@
 
         lax.fori_loop(0, COLS // 2, body, 0)
 
-    depth_forward(False, send_c, 0)
-    pl.semaphore_wait(barrier, DEVICES - 1)
-    exchange(functools.partial(forward_block, send_c, 0, 0), 0)
-    depth_forward(False, send_c, 1)
-    exchange(functools.partial(forward_block, send_c, 0, 1), 1)
+    def forward_stage(stage):
+        sends = send_c if stage < 2 else send_q
+        return functools.partial(forward_block, sends, stage // 2, stage % 2)
+
+    for stage in range(4):
+        depth_forward(stage >= 2, send_c if stage < 2 else send_q, stage % 2)
+        if stage == 0:
+            pl.semaphore_wait(barrier, DEVICES - 1)
+        keep_own(forward_stage(stage), stage)
+        exchange(forward_stage(stage), stage, FIRST)
+    for stage in range(4):
+        exchange(forward_stage(stage), stage, 1 - FIRST)
+    multipliers()
+    loads[3].wait()
     for h in range(2):
-        depth_forward(True, send_q, h)
-        exchange(functools.partial(forward_block, send_q, 1, h), 2 + h)
-    multipliers()
-    for h in range(2):
-        arrived(functools.partial(forward_block, send_c, 0, h), h)
+        arrived(forward_stage(h), h)
         second_forward(0, h)
     first_forward_conc()
     mass = jnp.broadcast_to(plane[0, 0:1, 0:1], (128, 256)) * (1.0 / TOTAL)
     for h in range(2):
-        arrived(functools.partial(forward_block, send_q, 1, h), 2 + h)
+        arrived(forward_stage(2 + h), 2 + h)
         second_forward(1, h)
     combine_and_first_inverse()
     for h in range(2):
+        block = functools.partial(backward_block, h)
         second_inverse(h, mass)
-        exchange(functools.partial(backward_block, h), 4 + h)
-    outs = []
+        keep_own(block, 4 + h)
+        for core in range(2):
+            exchange(block, 4 + h, core)
     for h in range(2):
         arrived(functools.partial(backward_block, h), 4 + h)
         depth_inverse(h)
-        rows = pl.ds(h * HALF * COLS, HALF * COLS)
-        for i in range(2):
-            outs.append(
-                pltpu.make_async_copy(
-                    out.at[i, rows, :],
-                    out_hbm.at[rows, i * 128 : (i + 1) * 128],
-                    out_sem.at[h, i],
-                )
-            )
-            outs[-1].start()
     mass_ref[...] = got[0, 8:16, :]
-    for copy in outs:
+
+
+def deliver(parts_ref, mass_in, out_hbm, mass_ref, sem):
+    copies = [
+        pltpu.make_async_copy(
+            parts_ref.at[i], out_hbm.at[:, i * 128 : (i + 1) * 128], sem.at[i]
+        )
+        for i in range(2)
+    ]
+    for copy in copies:
+        copy.start()
+    mass_ref[...] = mass_in[0:1, 0:1]
+    for copy in copies:
         copy.wait()
 
 
 def local(concentration):
-    zf, zi = depth_tables()
-    pf, pt = plane_tables()
+    tables = all_tables()
     anywhere = pl.BlockSpec(memory_space=pl.ANY)
-    updated, mass = pl.pallas_call(
+    vmem = pl.BlockSpec(memory_space=pltpu.VMEM)
+    halves, mass = pl.pallas_call(
         kernel,
         out_shape=(
-            jax.ShapeDtypeStruct((ROWS * COLS, NZ), f32),
+            jax.ShapeDtypeStruct((2, ROWS * COLS, 128), f32),
             jax.ShapeDtypeStruct((8, 128), f32),
         ),
-        in_specs=[anywhere] * 5,
-        out_specs=(anywhere, pl.BlockSpec(memory_space=pltpu.VMEM)),
+        in_specs=[anywhere] * 2,
+        out_specs=(vmem, vmem),
         scratch_shapes=[
             pltpu.VMEM((2, ROWS * COLS, 128), f32),
-            pltpu.VMEM(zf.shape, bf16),
-            pltpu.VMEM(zi.shape, bf16),
-            pltpu.VMEM(pf.shape, bf16),
-            pltpu.VMEM(pt.shape, bf16),
+            pltpu.VMEM(tables.shape, bf16),
             pltpu.VMEM((2, KEPT * 16, HALF), f32),
             pltpu.VMEM((2, KEPT * 16, HALF), f32),
             pltpu.VMEM((4, NY, NX), f32),
             pltpu.VMEM((2, NY, NX), f32),
             pltpu.VMEM((2, KEPT * 16, HALF), f32),
-            pltpu.VMEM((2, ROWS * COLS, 128), f32),
             pltpu.VMEM((NY, NX), f32),
             pltpu.VMEM((NY, NX), f32),
-            pltpu.SemaphoreType.DMA((6,)),
-            pltpu.SemaphoreType.DMA((2, 2)),
+            pltpu.SemaphoreType.DMA((4,)),
             pltpu.SemaphoreType.DMA((6,)),
             pltpu.SemaphoreType.DMA((6,)),
             pltpu.SemaphoreType.DMA((6,)),
         ],
         compiler_params=pltpu.CompilerParams(
-            collective_id=0, has_side_effects=True, vmem_limit_bytes=56 * 2**20
+            collective_id=0, has_side_effects=True, vmem_limit_bytes=50 * 2**20
         ),
         name="cahn_hilliard_step",
     )(
         concentration.reshape(ROWS * COLS, NZ),
-        jnp.asarray(zf), jnp.asarray(zi), jnp.asarray(pf), jnp.asarray(pt),
+        jnp.asarray(tables),
     )
-    return updated.reshape(ROWS, COLS, NZ), mass[0, 0]
+    updated, mass = pl.pallas_call(
+        deliver,
+        out_shape=(
+            jax.ShapeDtypeStruct((ROWS * COLS, NZ), f32),
+            jax.ShapeDtypeStruct((1, 1), f32),
+        ),
+        in_specs=[vmem, vmem],
+        out_specs=(anywhere, vmem),
+        scratch_shapes=[pltpu.SemaphoreType.DMA((2,))],
+        compiler_params=pltpu.CompilerParams(vmem_limit_bytes=8 * 2**20),
+        name="deliver",
+    )(halves, mass)
+    return updated.reshape(ROWS, COLS, NZ), mass.reshape(())
 
 
 def solution(mesh):

time: 99.3 us -> 90.2 us (0.908)
  the two profiles are of different devices: /device:TPU:0 before, /device:TPU:1 now
where the time goes in v3:
time: 90.2 us; the launch traced here: 90.1 us
  Pallas kernels  89.4 us (99%)
    pallas_call x1, Pallas kernels, local(): pl.pallas_call(kernel, out_shape=(jax.ShapeDtypeStruct((2, ROWS * COLS, 1...  87.6 us
    pallas_call x1, Pallas kernels, local(): pl.pallas_call(deliver, out_shape=(jax.ShapeDtypeStruct((ROWS * COLS, NZ)...  1.84 us

profile of v3, /device:TPU:1, one launch (start us, length us, event | category | flops | bytes accessed | tf_op | source)
XLA Modules:
  0.0 90.1 jit_solution(10054532809827793666)
XLA Ops:
  0.6 87.6 %cahn_hilliard_step.1 = (f32[2,2048,128]{2,1,0:T(8,128)S(1)}, f32[8,128]{1,0:T(8,128)S(1)}) custom-call(f32[2048,256]{1,0:T(8,128)} %bitcast.3, bf16[20,256,256]{2,1,0:T(8,128)(2,1)} %constant.2.clone.tables_hbm), custom_call_target="tpu_custom_call" | custom-call | tf_op jit(solution)/shard_map/cahn_hilliard_step/pallas_call | solution.py:408
  88.2 1.8 %deliver.1 = (f32[2048,256]{1,0:T(8,128)}, f32[1,1]{1,0:T(1,128)}) custom-call(f32[2,2048,128]{2,1,0:T(8,128)S(1)} %get-tuple-element.6.parts_ref, f32[8,128]{1,0:T(8,128)S(1)} %get-tuple-element.7.mass_in), custom_call_target="tpu_custom_call" | custom-call | tf_op jit(solution)/shard_map/deliver/pallas_call | solution.py:439

commit v4 on v3

--- a/solution.py
+++ b/solution.py
@@ -228,11 +228,9 @@
         def _():
             send(slab, 2 * chip + core)
 
-    def arrived(block, stage):
-        src, dst = block(slab, pencil)
-        pltpu.make_async_copy(src, dst, local_sem.at[stage]).wait()
+    def everything(stage):
         rows = pl.ds(0, 16 * (DEVICES - 1))
-        everything = pltpu.make_async_remote_copy(
+        return pltpu.make_async_remote_copy(
             src_ref=got.at[0, rows, :],
             dst_ref=got.at[0, rows, :],
             send_sem=send_sem.at[stage],
@@ -240,7 +238,11 @@
             device_id=(slab, pencil),
             device_id_type=MESH,
         )
-        everything.wait()
+
+    def arrived(block, stage):
+        src, dst = block(slab, pencil)
+        pltpu.make_async_copy(src, dst, local_sem.at[stage]).wait()
+        everything(stage).wait_recv()
 
     def lane_halves(h):
         return [slice(i * ROWS + h * HALF, i * ROWS + (h + 1) * HALF) for i in range(2)]
@@ -350,7 +352,7 @@
                     ]
             return carry
 
-        lax.fori_loop(0, COLS // 2, body, 0)
+        lax.fori_loop(0, COLS // 2, body, 0, unroll=True)
 
     def forward_stage(stage):
         sends = send_c if stage < 2 else send_q
@@ -385,6 +387,8 @@
         arrived(functools.partial(backward_block, h), 4 + h)
         depth_inverse(h)
     mass_ref[...] = got[0, 8:16, :]
+    for stage in range(6):
+        everything(stage).wait_send()
 
 
 def deliver(parts_ref, mass_in, out_hbm, mass_ref, sem):

time: 90.2 us -> 85.7 us (0.950)
  Pallas kernels: 89.4 us -> 85 us
    pallas_call x1, Pallas kernels: 87.6 us -> 83.1 us  [local(): pl.pallas_call(kernel, out_shape=(jax.ShapeDtypeStruct((2, ROWS * COLS, 1...]
where the time goes in v4:
time: 85.7 us; the launch traced here: 85.6 us
  Pallas kernels  85 us (99%)
    pallas_call x1, Pallas kernels, local(): pl.pallas_call(kernel, out_shape=(jax.ShapeDtypeStruct((2, ROWS * COLS, 1...  83.1 us
    pallas_call x1, Pallas kernels, local(): pl.pallas_call(deliver, out_shape=(jax.ShapeDtypeStruct((ROWS * COLS, NZ)...  1.84 us

profile of v4, /device:TPU:1, one launch (start us, length us, event | category | flops | bytes accessed | tf_op | source)
XLA Modules:
  0.0 85.6 jit_solution(5917329017632144577)
XLA Ops:
  0.6 83.1 %cahn_hilliard_step.1 = (f32[2,2048,128]{2,1,0:T(8,128)S(1)}, f32[8,128]{1,0:T(8,128)S(1)}) custom-call(f32[2048,256]{1,0:T(8,128)} %bitcast.3, bf16[20,256,256]{2,1,0:T(8,128)(2,1)} %constant.2.clone.tables_hbm), custom_call_target="tpu_custom_call" | custom-call | tf_op jit(solution)/shard_map/cahn_hilliard_step/pallas_call | solution.py:412
  83.8 1.8 %deliver.1 = (f32[2048,256]{1,0:T(8,128)}, f32[1,1]{1,0:T(1,128)}) custom-call(f32[2,2048,128]{2,1,0:T(8,128)S(1)} %get-tuple-element.6.parts_ref, f32[8,128]{1,0:T(8,128)S(1)} %get-tuple-element.7.mass_in), custom_call_target="tpu_custom_call" | custom-call | tf_op jit(solution)/shard_map/deliver/pallas_call | solution.py:443

commit v5 on v4

--- a/solution.py
+++ b/solution.py
@@ -18,6 +18,7 @@
 COLS = 8
 HALF = ROWS // 2
 TOTAL = NX * NY * NZ
+NEAR_LAST = [22, 23, 13, 14, 15, 26, 6, 17, 18, 29, 19, 30, 20, 31, 10, 21, 11, 12, 2, 25, 5, 16, 27, 28, 7, 9, 1, 24, 3, 4, 8]
 FIRST = 1
 
 time_step = 1.0
@@ -173,7 +174,7 @@
                     ]
             return carry
 
-        lax.fori_loop(0, COLS // 2, body, 0)
+        lax.fori_loop(0, COLS // 2, body, 0, unroll=True)
 
     def forward_block(sends, field, h, to_slab, to_pencil):
         return (
@@ -221,7 +222,13 @@
             send(1 - slab, to_pencil)
             return carry
 
-        lax.fori_loop(1, 32, pair, 0)
+        if stage < 4:
+            lax.fori_loop(1, 32, pair, 0)
+        else:
+            for turn in NEAR_LAST:
+                to_pencil = 2 * lax.rem(chip + turn, 32) + core
+                send(1 - slab, to_pencil)
+                send(slab, to_pencil)
         send(1 - slab, 2 * chip + core)
 
         @pl.when(lax.rem(pencil, 2) != core)
@@ -381,8 +388,9 @@
         block = functools.partial(backward_block, h)
         second_inverse(h, mass)
         keep_own(block, 4 + h)
-        for core in range(2):
-            exchange(block, 4 + h, core)
+        exchange(block, 4 + h, FIRST)
+    for h in range(2):
+        exchange(functools.partial(backward_block, h), 4 + h, 1 - FIRST)
     for h in range(2):
         arrived(functools.partial(backward_block, h), 4 + h)
         depth_inverse(h)
@@ -394,8 +402,11 @@
 def deliver(parts_ref, mass_in, out_hbm, mass_ref, sem):
     copies = [
         pltpu.make_async_copy(
-            parts_ref.at[i], out_hbm.at[:, i * 128 : (i + 1) * 128], sem.at[i]
-        )
+            parts_ref.at[i, r * 512 : (r + 1) * 512, :],
+            out_hbm.at[r * 512 : (r + 1) * 512, i * 128 : (i + 1) * 128],
+            sem.at[i, r],
+        )
+        for r in range(4)
         for i in range(2)
     ]
     for copy in copies:
@@ -448,7 +459,7 @@
         ),
         in_specs=[vmem, vmem],
         out_specs=(anywhere, vmem),
-        scratch_shapes=[pltpu.SemaphoreType.DMA((2,))],
+        scratch_shapes=[pltpu.SemaphoreType.DMA((2, 4))],
         compiler_params=pltpu.CompilerParams(vmem_limit_bytes=8 * 2**20),
         name="deliver",
     )(halves, mass)

time: 85.7 us -> 84.3 us (0.984)
  the two profiles are of different devices: /device:TPU:1 before, /device:TPU:0 now
where the time goes in v5:
time: 84.3 us; the launch traced here: 84.2 us
  Pallas kernels  83.6 us (99%)
    pallas_call x1, Pallas kernels, local(): pl.pallas_call(kernel, out_shape=(jax.ShapeDtypeStruct((2, ROWS * COLS, 1...  81.7 us
    pallas_call x1, Pallas kernels, local(): pl.pallas_call(deliver, out_shape=(jax.ShapeDtypeStruct((ROWS * COLS, NZ)...  1.89 us

profile of v5, /device:TPU:0, one launch (start us, length us, event | category | flops | bytes accessed | tf_op | source)
XLA Modules:
  0.0 84.2 jit_solution(14327906631979165876)
XLA Ops:
  0.6 81.7 %cahn_hilliard_step.1 = (f32[2,2048,128]{2,1,0:T(8,128)S(1)}, f32[8,128]{1,0:T(8,128)S(1)}) custom-call(f32[2048,256]{1,0:T(8,128)} %bitcast.3, bf16[20,256,256]{2,1,0:T(8,128)(2,1)} %constant.2.clone.tables_hbm), custom_call_target="tpu_custom_call" | custom-call | tf_op jit(solution)/shard_map/cahn_hilliard_step/pallas_call | solution.py:423
  82.4 1.9 %deliver.1 = (f32[2048,256]{1,0:T(8,128)}, f32[1,1]{1,0:T(1,128)}) custom-call(f32[2,2048,128]{2,1,0:T(8,128)S(1)} %get-tuple-element.6.parts_ref, f32[8,128]{1,0:T(8,128)S(1)} %get-tuple-element.7.mass_in), custom_call_target="tpu_custom_call" | custom-call | tf_op jit(solution)/shard_map/deliver/pallas_call | solution.py:454

commit v6 on v5

--- a/solution.py
+++ b/solution.py
@@ -19,7 +19,7 @@
 HALF = ROWS // 2
 TOTAL = NX * NY * NZ
 NEAR_LAST = [22, 23, 13, 14, 15, 26, 6, 17, 18, 29, 19, 30, 20, 31, 10, 21, 11, 12, 2, 25, 5, 16, 27, 28, 7, 9, 1, 24, 3, 4, 8]
-FIRST = 1
+FIRST = 0
 
 time_step = 1.0
 stiffness = 1.0
@@ -388,9 +388,8 @@
         block = functools.partial(backward_block, h)
         second_inverse(h, mass)
         keep_own(block, 4 + h)
-        exchange(block, 4 + h, FIRST)
-    for h in range(2):
-        exchange(functools.partial(backward_block, h), 4 + h, 1 - FIRST)
+        exchange(block, 4 + h, 1)
+        exchange(block, 4 + h, 0)
     for h in range(2):
         arrived(functools.partial(backward_block, h), 4 + h)
         depth_inverse(h)

time: 84.3 us -> 84.2 us (level)
  no operation moved by 1% of the time
where the time goes in v6:
time: 84.2 us; the launch traced here: 84.1 us
  Pallas kernels  83.4 us (99%)
    pallas_call x1, Pallas kernels, local(): pl.pallas_call(kernel, out_shape=(jax.ShapeDtypeStruct((2, ROWS * COLS, 1...  81.5 us
    pallas_call x1, Pallas kernels, local(): pl.pallas_call(deliver, out_shape=(jax.ShapeDtypeStruct((ROWS * COLS, NZ)...  1.89 us

profile of v6, /device:TPU:0, one launch (start us, length us, event | category | flops | bytes accessed | tf_op | source)
XLA Modules:
  0.0 84.1 jit_solution(14341627404534966487)
XLA Ops:
  0.6 81.5 %cahn_hilliard_step.1 = (f32[2,2048,128]{2,1,0:T(8,128)S(1)}, f32[8,128]{1,0:T(8,128)S(1)}) custom-call(f32[2048,256]{1,0:T(8,128)} %bitcast.3, bf16[20,256,256]{2,1,0:T(8,128)(2,1)} %constant.2.clone.tables_hbm), custom_call_target="tpu_custom_call" | custom-call | tf_op jit(solution)/shard_map/cahn_hilliard_step/pallas_call | solution.py:422
  82.2 1.9 %deliver.1 = (f32[2048,256]{1,0:T(8,128)}, f32[1,1]{1,0:T(1,128)}) custom-call(f32[2,2048,128]{2,1,0:T(8,128)S(1)} %get-tuple-element.6.parts_ref, f32[8,128]{1,0:T(8,128)S(1)} %get-tuple-element.7.mass_in), custom_call_target="tpu_custom_call" | custom-call | tf_op jit(solution)/shard_map/deliver/pallas_call | solution.py:453

commit v7 on v6

--- a/solution.py
+++ b/solution.py
@@ -310,7 +310,7 @@
 
     def combine_and_first_inverse():
         def body(i, carry):
-            rows = row_block(i)
+            rows = pl.ds(pl.multiple_of(i * 256, 256), 256)
             vr, vi = [], []
             for d, cube in enumerate(first_forward(1, rows)):
                 lanes = slice(d * 128, (d + 1) * 128)
@@ -329,7 +329,7 @@
                 plane[3, rows, a * 128 : (a + 1) * 128] = xi
             return carry
 
-        lax.fori_loop(0, 4, body, 0)
+        lax.fori_loop(0, 2, body, 0)
 
     def second_inverse(h, mass):
         quarters = [slice(a * 128, (a + 1) * 128) for a in range(4)]

time: 84.2 us -> 84.2 us (level)
  no operation moved by 1% of the time
where the time goes in v7:
time: 84.2 us; the launch traced here: 84.1 us
  Pallas kernels  83.4 us (99%)
    pallas_call x1, Pallas kernels, local(): pl.pallas_call(kernel, out_shape=(jax.ShapeDtypeStruct((2, ROWS * COLS, 1...  81.5 us
    pallas_call x1, Pallas kernels, local(): pl.pallas_call(deliver, out_shape=(jax.ShapeDtypeStruct((ROWS * COLS, NZ)...  1.89 us

profile of v7, /device:TPU:0, one launch (start us, length us, event | category | flops | bytes accessed | tf_op | source)
XLA Modules:
  0.0 84.1 jit_solution(10299250306668780577)
XLA Ops:
  0.6 81.5 %cahn_hilliard_step.1 = (f32[2,2048,128]{2,1,0:T(8,128)S(1)}, f32[8,128]{1,0:T(8,128)S(1)}) custom-call(f32[2048,256]{1,0:T(8,128)} %bitcast.3, bf16[20,256,256]{2,1,0:T(8,128)(2,1)} %constant.2.clone.tables_hbm), custom_call_target="tpu_custom_call" | custom-call | tf_op jit(solution)/shard_map/cahn_hilliard_step/pallas_call | solution.py:422
  82.2 1.9 %deliver.1 = (f32[2048,256]{1,0:T(8,128)}, f32[1,1]{1,0:T(1,128)}) custom-call(f32[2,2048,128]{2,1,0:T(8,128)S(1)} %get-tuple-element.6.parts_ref, f32[8,128]{1,0:T(8,128)S(1)} %get-tuple-element.7.mass_in), custom_call_target="tpu_custom_call" | custom-call | tf_op jit(solution)/shard_map/deliver/pallas_call | solution.py:453
